TPU v7x, 512 devices: a whole 4x8x8 slice. The times are simulated.
512 devices in a mesh: gx: 64 (over y, z), gy: 8 (over x, core).
Axes of the slice: x: 4, y: 8, z: 8, core: 2. Of those that a mesh axis runs over, the one named last changes fastest.
Arguments:
- droplets: float32 [2, 32, 128, 4096], P(None, None, 'gx', 'gy'), as said below
- moves: int32 [2, 32, 128, 4096], P(None, None, 'gx', 'gy'), may hold values from 0 to 8, as said below
- pairing: int32 [2, 32, 128, 4096], P(None, None, 'gx', 'gy'), may hold values from 0 to 31, as said below
- collisions: int32 [2, 16, 128, 4096], P(None, None, 'gx', 'gy'), may hold values from 0 to 3
Outputs:
- droplets_out: float32 [2, 32, 128, 4096], P(None, None, 'gx', 'gy')
- moments: float32 [2, 2, 16], replicated
Inputs may be any that keep to these rules, and one draw needn't show every extreme that they name: `droplets`: entry 0 holds whole-number multiplicities from 24 to below 300, entry 1 masses from 0.05 to 2. `moves`: A code c means a step of c // 3 - 1 along x and c % 3 - 1 along y. In each step, slot and level, all droplets of one y-row take the same x-step and all droplets landing in one x-column take the same y-step, so every cell and slot receives exactly one droplet. `pairing`: for each step and cell, the entries along the slot dimension are a permutation of 0 to 31.
All inputs are finite; a program needn't handle non-finite values.
Results may differ from a plain program's by a relative error of at most 0.0003.
Values sent between devices are 32-bit elements; how exact they have to be, the bound alone decides.
A program may use at most 64 MiB of HBM per device.

v0:
```python
import jax
import jax.numpy as jnp
from jax import lax
from jax.sharding import Mesh
from jax.sharding import PartitionSpec as P

LEVELS = 16
GY = ("gy_0", "gy_1")
GX = ("gx_0", "gx_1")
GX_GY = ("gx_0", "gx_1", "gy_0", "gy_1")


count_unit = 4096.0


def padded(array, sides, width):
    for axis, dim in sides:
        size, length = (lax.axis_size(axis), array.shape[dim])
        up = [(i, (i + 1) % size) for i in range(size)]
        down = [(j, i) for i, j in up]
        last = lax.slice_in_dim(array, length - width, length, axis=dim)
        leading = lax.slice_in_dim(array, 0, width, axis=dim)
        before = lax.ppermute(last, axis, up)
        after = lax.ppermute(leading, axis, down)
        array = jnp.concatenate([before, array, after], axis=dim)
    return array


def over_axes(array, axes):
    for axis in axes:
        array = lax.psum(array, axis)
    return array


def spread(state, codes):
    twos, slots, cols, rows, levels = state.shape
    extended = jnp.zeros((twos, slots, cols + 2, rows + 2, levels), state.dtype)
    for direction in range(9):
        step_x = direction // 3 - 1
        step_y = direction % 3 - 1
        chosen = jnp.where((codes == direction)[None], state, jnp.zeros_like(state))
        extended = extended + jnp.pad(
            chosen, ((0, 0), (0, 0), (1 + step_x, 1 - step_x), (1 + step_y, 1 - step_y), (0, 0))
        )
    return extended


def settle(extended, cols, rows):
    twos, slots, wide, tall, levels = extended.shape
    rims = jnp.stack([extended[:, :, :, 0], extended[:, :, :, rows + 1]], axis=2).reshape(
        twos, slots, 2, (cols + 2) * levels
    )
    got = padded(rims, ((GY, 2),), 1).reshape(twos, slots, 4, cols + 2, levels)
    middle = (
        extended[:, :, :, 1 : rows + 1]
        .at[:, :, :, 0]
        .add(got[:, :, 0])
        .at[:, :, :, rows - 1]
        .add(got[:, :, 3])
    )
    rims = jnp.stack([middle[:, :, 0], middle[:, :, cols + 1]], axis=2).reshape(
        twos, slots, 2, rows * levels
    )
    got = padded(rims, ((GX, 2),), 1).reshape(twos, slots, 4, rows, levels)
    block = (
        middle[:, :, 1 : cols + 1]
        .at[:, :, 0]
        .add(got[:, :, 0])
        .at[:, :, cols - 1]
        .add(got[:, :, 3])
    )
    return block


def collide(first_count, second_count, first_mass, second_mass, tries):
    big_first = first_count >= second_count
    larger = jnp.where(big_first, first_count, second_count)
    smaller = jnp.where(big_first, second_count, first_count)
    larger_mass = jnp.where(big_first, first_mass, second_mass)
    smaller_mass = jnp.where(big_first, second_mass, first_mass)
    taken = jnp.minimum(tries, larger // smaller)
    remain = larger - taken * smaller
    splits = remain == 0
    halved = smaller // 2
    larger_new = jnp.where(splits, halved, remain)
    smaller_new = jnp.where(splits, smaller - halved, smaller)
    grown = smaller_mass + taken.astype(first_mass.dtype) * larger_mass
    larger_mass_new = jnp.where(splits, grown, larger_mass)
    first_new = jnp.where(big_first, larger_new, smaller_new)
    second_new = jnp.where(big_first, smaller_new, larger_new)
    first_mass_new = jnp.where(big_first, larger_mass_new, grown)
    second_mass_new = jnp.where(big_first, grown, larger_mass_new)
    return (first_new, second_new, first_mass_new, second_mass_new)


def pair_column(counts_f, masses, order, tries):
    slots = counts_f.shape[0]
    slot_ids = lax.broadcasted_iota(jnp.int32, (slots, slots, 1), 1)
    hits = order[:, None, :] == slot_ids
    counts = counts_f.astype(jnp.int32)
    counts_p = jnp.sum(jnp.where(hits, counts[None], 0), axis=1)
    masses_p = jnp.sum(jnp.where(hits, masses[None], jnp.zeros_like(masses)[None]), axis=1)
    first_new, second_new, first_mass, second_mass = collide(
        counts_p[0::2], counts_p[1::2], masses_p[0::2], masses_p[1::2], tries
    )
    counts_pair = jnp.stack([first_new, second_new], axis=1).reshape(counts_p.shape)
    masses_pair = jnp.stack([first_mass, second_mass], axis=1).reshape(masses_p.shape)
    counts_new = jnp.sum(jnp.where(hits, counts_pair[:, None], 0), axis=0)
    masses_new = jnp.sum(
        jnp.where(hits, masses_pair[:, None], jnp.zeros_like(masses_pair)[:, None]), axis=0
    )
    return (counts_new.astype(counts_f.dtype), masses_new)


def coalesce(block, order, tries):
    twos, slots, cols, rows, levels = block.shape
    flat = block.reshape(twos, slots, cols, rows * levels)
    results = []
    for column in range(cols):
        counts_new, masses_new = pair_column(
            flat[0, :, column], flat[1, :, column], order[:, column], tries[:, column]
        )
        results.append(jnp.stack([counts_new, masses_new]))
    return jnp.stack(results, axis=2).reshape(block.shape)


def shards(droplets, moves, pairing, collisions):
    twos, slots, cols, flat = droplets.shape
    levels = LEVELS
    rows = flat // levels
    state = droplets.reshape(twos, slots, cols, rows, levels)
    totals = []
    for step in range(moves.shape[0]):
        codes = moves[step].reshape(slots, cols, rows, levels)
        state = settle(spread(state, codes), cols, rows)
        state = coalesce(state, pairing[step], collisions[step])
        count_sum = jnp.sum(state[0], axis=(0, 1, 2))
        liquid_sum = jnp.sum(state[0] * state[1], axis=(0, 1, 2))
        terms = jnp.stack([count_sum, liquid_sum])
        totals.append(over_axes(terms, GX_GY))
    summed = jnp.stack(totals)
    cells_x = cols * lax.axis_size(GX)
    cells_y = rows * lax.axis_size(GY)
    moments = summed / (cells_x * cells_y * count_unit)
    return (state.reshape(droplets.shape), moments)


def solution(mesh):
    torus = Mesh(mesh.devices.reshape(8, 8, 4, 2), ("gx_0", "gx_1", "gy_0", "gy_1"))
    placed = (
        P(None, None, GX, GY),
        P(None, None, GX, GY),
        P(None, None, GX, GY),
        P(None, None, GX, GY),
    )
    return jax.shard_map(
        shards, mesh=torus, in_specs=placed, out_specs=(P(None, None, GX, GY), P()), check_vma=False
    )
```

profile of v0, /device:TPU:1, one launch (start us, length us, event | category | flops | bytes accessed | tf_op | source)
XLA Modules:
  0.0 132.2 jit_solution(4844064748951774139)
XLA Ops:
  0.6 1.0 fusion.55
  1.9 0.8 broadcast_compare_fusion.16
  3.1 1.2 broadcast_select_fusion.17
  4.3 0.6 pad_add_fusion.1
  4.9 0.7 fusion.50
  5.6 2.6 %collective-permute-start = (f32[2,32,1,64]{1,3,0,2:T(8,128)}, f32[2,32,1,64]{1,3,0,2:T(8,128)}, u32[]{:S(2)}, u32[]{:S(2)}) collective-permute-start(f32[2,32,1,64]{1,3,0,2:T(8,128)} %bitcast.13), channel_id=1, source_target_pairs={{0,1},{1,2},{2,3},{3,4},{4,5},{5,6},{6,7},{7,0},{8,9},{9,10},{10,1... | collective-permute-start | bytes 49160 | tf_op jit(solution)/shard_map/ppermute | solution.py:23
  8.1 4.3 %collective-permute-start.1 = (f32[2,32,1,64]{1,3,0,2:T(8,128)}, f32[2,32,1,64]{1,3,0,2:T(8,128)}, u32[]{:S(2)}, u32[]{:S(2)}) collective-permute-start(f32[2,32,1,64]{1,3,0,2:T(8,128)} %bitcast.16), channel_id=1, source_target_pairs={{1,0},{2,1},{3,2},{4,3},{5,4},{6,5},{7,6},{0,7},{9,8},{10,9},{11,1... | collective-permute-start | bytes 49160 | tf_op jit(solution)/shard_map/ppermute | solution.py:24
  12.4 0.7 slice_bitcast_fusion.5
  13.3 1.5 %broadcast_compare_fusion.17 = (pred[1,32,2,512]{1,3,2,0:T(8,128)(4,1)}, pred[1,32,2,512]{1,3,2,0:T(8,128)(4,1)S(1)}, pred[1,32,2,512]{1,3,2,0:T(8,128)(4,1)S(1)...) fusion(s32[1,32,2,512]{1,3,2,0:T(8,128)S(1)} %copy.114), kind=kLoop, calls=%fused_computation.87 | loop fusion | flops 294912 | bytes 425984 | tf_op jit(solution)/shard_map/eq | solution.py:41
  14.8 1.3 %fusion.56 = (s32[32,1,512]{2,1,0:T(1,128)S(1)}, s32[32,1,512]{2,1,0:T(1,128)S(1)}, s32[32,1,512]{2,1,0:T(1,128)S(1)}, s32[32,1,512]{2,1,0:T(1,128)S(1)}) fusion(s32[32,2,512]{2,1,0:T(2,128)} %get-tuple-element.172, s32[32,2,512]{2,1,0:T(2,128)} %get-tuple-element.173), kind=kLoop, calls=%fused_computation.232 | loop fusion | bytes 524288 | tf_op jit(solution)/shard_map/slice | solution.py:121
  16.1 0.9 fusion.57
  17.2 0.8 fusion.18
  18.1 0.9 fusion.17
  19.2 1.9 %collective-permute-start.2 = (f32[2,32,1,512]{1,3,2,0:T(8,128)S(1)}, f32[2,32,1,512]{1,3,2,0:T(8,128)S(1)}, u32[]{:S(2)}, u32[]{:S(2)}) collective-permute-start(f32[2,32,1,512]{1,3,2,0:T(8,128)S(1)} %get-tuple-element.144), channel_id=1, source_target_pairs={{0,8},{8,16},{16,24},{24,32},{32,40},{40,48},{48,56},{56,64},{64,7... | collective-permute-start | bytes 393224 | tf_op jit(solution)/shard_map/ppermute | solution.py:23
  21.3 9.5 %collective-permute-start.3 = (f32[2,32,1,512]{1,3,2,0:T(8,128)S(1)}, f32[2,32,1,512]{1,3,2,0:T(8,128)S(1)}, u32[]{:S(2)}, u32[]{:S(2)}) collective-permute-start(f32[2,32,1,512]{1,3,2,0:T(8,128)S(1)} %get-tuple-element.143), channel_id=1, source_target_pairs={{8,0},{16,8},{24,16},{32,24},{40,32},{48,40},{56,48},{64,56},{72,6... | collective-permute-start | bytes 393224 | tf_op jit(solution)/shard_map/ppermute | solution.py:24
  30.8 8.2 %collective-permute-done.2 = f32[2,32,1,512]{1,3,2,0:T(8,128)S(1)} collective-permute-done((f32[2,32,1,512]{1,3,2,0:T(8,128)S(1)}, f32[2,32,1,512]{1,3,2,0:T(8,128)S(1)}, u32[]{:S(2)}, u32[]{:S(2)}) %collective-permute-start.2) | collective-permute-done | bytes 131104 | tf_op jit(solution)/shard_map/ppermute | solution.py:23
  39.0 0.9 collective-permute-done.3
  40.3 0.4 select_reduce_fusion.11
  40.9 0.4 select_reduce_fusion.15
  41.4 0.4 select_reduce_fusion.9
  42.0 0.4 select_reduce_fusion.13
  42.5 0.8 select_bitcast_fusion.7
  43.8 0.7 fusion.19
  44.7 0.4 select_reduce_fusion.12
  45.2 0.4 select_reduce_fusion.10
  45.5 0.6 convert_bitcast_fusion.2
  48.3 0.6 pad_add_fusion
  48.9 3.8 %collective-permute-start.4 = (f32[2,32,1,64]{1,3,0,2:T(8,128)S(1)}, f32[2,32,1,64]{1,3,0,2:T(8,128)S(1)}, u32[]{:S(2)}, u32[]{:S(2)}) collective-permute-start(f32[2,32,1,64]{1,3,0,2:T(8,128)S(1)} %bitcast.263), channel_id=1, source_target_pairs={{0,1},{1,2},{2,3},{3,4},{4,5},{5,6},{6,7},{7,0},{8,9},{9,10},{10,1... | collective-permute-start | bytes 49160 | tf_op jit(solution)/shard_map/ppermute | solution.py:23
  52.9 1.2 collective-permute-done.4
  54.1 2.3 %collective-permute-done.5 = f32[2,32,1,64]{1,3,0,2:T(8,128)S(1)} collective-permute-done((f32[2,32,1,64]{1,3,0,2:T(8,128)S(1)}, f32[2,32,1,64]{1,3,0,2:T(8,128)S(1)}, u32[]{:S(2)}, u32[]{:S(2)}) %collective-permute-start.5) | collective-permute-done | bytes 16416 | tf_op jit(solution)/shard_map/ppermute | solution.py:24
  56.6 0.9 fusion.53
  57.5 1.9 %collective-permute-start.6 = (f32[2,32,1,512]{1,3,2,0:T(8,128)}, f32[2,32,1,512]{1,3,2,0:T(8,128)S(1)}, u32[]{:S(2)}, u32[]{:S(2)}) collective-permute-start(f32[2,32,1,512]{1,3,2,0:T(8,128)} %get-tuple-element.129), channel_id=1, source_target_pairs={{0,8},{8,16},{16,24},{24,32},{32,40},{40,48},{48,56},{56,64},{64,7... | collective-permute-start | bytes 393224 | tf_op jit(solution)/shard_map/ppermute | solution.py:23
  59.8 7.7 %collective-permute-start.7 = (f32[2,32,1,512]{1,3,2,0:T(8,128)S(1)}, f32[2,32,1,512]{1,3,2,0:T(8,128)S(1)}, u32[]{:S(2)}, u32[]{:S(2)}) collective-permute-start(f32[2,32,1,512]{1,3,2,0:T(8,128)S(1)} %get-tuple-element.128), channel_id=1, source_target_pairs={{8,0},{16,8},{24,16},{32,24},{40,32},{48,40},{56,48},{64,56},{72,6... | collective-permute-start | bytes 393224 | tf_op jit(solution)/shard_map/ppermute | solution.py:24
  67.4 9.8 %collective-permute-done.6 = f32[2,32,1,512]{1,3,2,0:T(8,128)S(1)} collective-permute-done((f32[2,32,1,512]{1,3,2,0:T(8,128)}, f32[2,32,1,512]{1,3,2,0:T(8,128)S(1)}, u32[]{:S(2)}, u32[]{:S(2)}) %collective-permute-start.6) | collective-permute-done | bytes 131104 | tf_op jit(solution)/shard_map/ppermute | solution.py:23
  77.3 1.0 collective-permute-done.7
  78.6 0.4 select_reduce_fusion.3
  79.2 0.4 select_reduce_fusion.7
  79.8 0.4 select_reduce_fusion.1
  80.4 0.4 select_reduce_fusion.5
  80.8 0.8 select_bitcast_fusion.3
  81.7 0.4 select_reduce_fusion.6
  82.1 0.7 fusion.23
  84.6 0.9 copy.109
  85.6 10.7 %all-reduce.19 = (f32[2,16]{1,0:T(2,128)S(1)}, f32[2,16]{1,0:T(2,128)S(1)}) all-reduce(f32[2,16]{1,0:T(2,128)S(1)} %pad_maximum_fusion.9, f32[2,16]{1,0:T(2,128)S(1)} %pad_maximum_fusion.8), channel_id=1, replica_groups=mesh['gx_0'=8,'gx_1'=8,'gy_0'=4,'gy_1'=2] {'gx_0'}, use_global_device_ids=true, to_apply=%region_28.29 | all-reduce | flops 64 | bytes 512 | tf_op jit(solution)/shard_map/psum | solution.py:31
  96.2 16.4 %all-reduce.18 = (f32[2,16]{1,0:T(2,128)S(1)}, f32[2,16]{1,0:T(2,128)S(1)}) all-reduce(f32[2,16]{1,0:T(2,128)S(1)} %get-tuple-element.110, f32[2,16]{1,0:T(2,128)S(1)} %get-tuple-element.111), channel_id=1, replica_groups=mesh['gx_0'=8,'gx_1'=8,'gy_0'=4,'gy_1'=2] {'gx_1'}, use_global_device_ids=true, to_apply=%region_29.30 | all-reduce | flops 64 | bytes 512 | tf_op jit(solution)/shard_map/psum | solution.py:31
  112.7 7.5 %all-reduce.20 = (f32[2,16]{1,0:T(2,128)S(1)}, f32[2,16]{1,0:T(2,128)S(1)}) all-reduce(f32[2,16]{1,0:T(2,128)S(1)} %get-tuple-element.108, f32[2,16]{1,0:T(2,128)S(1)} %get-tuple-element.109), channel_id=1, replica_groups=mesh['gx_0'=8,'gx_1'=8,'gy_0'=4,'gy_1'=2] {'gy_0'}, use_global_device_ids=true, to_apply=%region_30.31 | all-reduce | flops 64 | bytes 512 | tf_op jit(solution)/shard_map/psum | solution.py:31
  120.1 11.4 %all-reduce.21 = (f32[1,2,16]{2,1,0:T(2,128)S(1)}, f32[1,2,16]{2,1,0:T(2,128)S(1)}) all-reduce(f32[1,2,16]{2,1,0:T(2,128)S(1)} %bitcast.268, f32[1,2,16]{2,1,0:T(2,128)S(1)} %bitcast.269), channel_id=1, replica_groups=mesh['gx_0'=8,'gx_1'=8,'gy_0'=4,'gy_1'=2] {'gy_1'}, use_global_device_ids=true, to_apply=%region_31.32 | all-reduce | flops 64 | bytes 512 | tf_op jit(solution)/shard_map/psum | solution.py:31
  131.6 0.6 maximum_multiply_fusion
  (121 shorter events, 8.1 us)
Async XLA Ops:
  0.6 2.1 %copy-start.3 = (f32[2,32,2,512]{3,2,1,0:T(2,128)S(1)}, f32[2,32,2,512]{3,2,1,0:T(2,128)}, u32[]{:S(2)}) copy-start(f32[2,32,2,512]{3,2,1,0:T(2,128)} %param.20) | copy-start | bytes 786436
  4.3 8.1 %copy-start.4 = (s32[2,32,2,512]{3,2,1,0:T(2,128)S(1)}, s32[2,32,2,512]{3,2,1,0:T(2,128)}, u32[]{:S(2)}) copy-start(s32[2,32,2,512]{3,2,1,0:T(2,128)} %param.22) | copy-start | bytes 786436
  5.6 11.7 %collective-permute-start = (f32[2,32,1,64]{1,3,0,2:T(8,128)}, f32[2,32,1,64]{1,3,0,2:T(8,128)}, u32[]{:S(2)}, u32[]{:S(2)}) collective-permute-start(f32[2,32,1,64]{1,3,0,2:T(8,128)} %bitcast.13), channel_id=1, source_target_pairs={{0,1},{1,2},{2,3},{3,4},{4,5},{5,6},{6,7},{7,0},{8,9},{9,10},{10,1... | collective-permute-start | bytes 49160 | tf_op jit(solution)/shard_map/ppermute | solution.py:23
  8.1 9.9 %collective-permute-start.1 = (f32[2,32,1,64]{1,3,0,2:T(8,128)}, f32[2,32,1,64]{1,3,0,2:T(8,128)}, u32[]{:S(2)}, u32[]{:S(2)}) collective-permute-start(f32[2,32,1,64]{1,3,0,2:T(8,128)} %bitcast.16), channel_id=1, source_target_pairs={{1,0},{2,1},{3,2},{4,3},{5,4},{6,5},{7,6},{0,7},{9,8},{10,9},{11,1... | collective-permute-start | bytes 49160 | tf_op jit(solution)/shard_map/ppermute | solution.py:24
  19.2 19.8 %collective-permute-start.2 = (f32[2,32,1,512]{1,3,2,0:T(8,128)S(1)}, f32[2,32,1,512]{1,3,2,0:T(8,128)S(1)}, u32[]{:S(2)}, u32[]{:S(2)}) collective-permute-start(f32[2,32,1,512]{1,3,2,0:T(8,128)S(1)} %get-tuple-element.144), channel_id=1, source_target_pairs={{0,8},{8,16},{16,24},{24,32},{32,40},{40,48},{48,56},{56,64},{64,7... | collective-permute-start | bytes 393224 | tf_op jit(solution)/shard_map/ppermute | solution.py:23
  21.3 18.7 %collective-permute-start.3 = (f32[2,32,1,512]{1,3,2,0:T(8,128)S(1)}, f32[2,32,1,512]{1,3,2,0:T(8,128)S(1)}, u32[]{:S(2)}, u32[]{:S(2)}) collective-permute-start(f32[2,32,1,512]{1,3,2,0:T(8,128)S(1)} %get-tuple-element.143), channel_id=1, source_target_pairs={{8,0},{16,8},{24,16},{32,24},{40,32},{48,40},{56,48},{64,56},{72,6... | collective-permute-start | bytes 393224 | tf_op jit(solution)/shard_map/ppermute | solution.py:24
  43.4 3.8 %copy-start = (pred[1,32,2,512]{1,3,2,0:T(8,128)(4,1)S(1)}, pred[1,32,2,512]{1,3,2,0:T(8,128)(4,1)}, u32[]{:S(2)}) copy-start(pred[1,32,2,512]{1,3,2,0:T(8,128)(4,1)} %get-tuple-element.154) | copy-start | bytes 98308
  43.4 3.8 %copy-start.1 = (pred[1,32,2,512]{1,3,2,0:T(8,128)(4,1)S(1)}, pred[1,32,2,512]{1,3,2,0:T(8,128)(4,1)}, u32[]{:S(2)}) copy-start(pred[1,32,2,512]{1,3,2,0:T(8,128)(4,1)} %get-tuple-element.161) | copy-start | bytes 98308
  43.4 3.8 %copy-start.2 = (pred[1,32,2,512]{1,3,2,0:T(8,128)(4,1)S(1)}, pred[1,32,2,512]{1,3,2,0:T(8,128)(4,1)}, u32[]{:S(2)}) copy-start(pred[1,32,2,512]{1,3,2,0:T(8,128)(4,1)} %get-tuple-element.162) | copy-start | bytes 98308
  48.9 5.2 %collective-permute-start.4 = (f32[2,32,1,64]{1,3,0,2:T(8,128)S(1)}, f32[2,32,1,64]{1,3,0,2:T(8,128)S(1)}, u32[]{:S(2)}, u32[]{:S(2)}) collective-permute-start(f32[2,32,1,64]{1,3,0,2:T(8,128)S(1)} %bitcast.263), channel_id=1, source_target_pairs={{0,1},{1,2},{2,3},{3,4},{4,5},{5,6},{6,7},{7,0},{8,9},{9,10},{10,1... | collective-permute-start | bytes 49160 | tf_op jit(solution)/shard_map/ppermute | solution.py:23
  52.7 3.7 %collective-permute-start.5 = (f32[2,32,1,64]{1,3,0,2:T(8,128)S(1)}, f32[2,32,1,64]{1,3,0,2:T(8,128)S(1)}, u32[]{:S(2)}, u32[]{:S(2)}) collective-permute-start(f32[2,32,1,64]{1,3,0,2:T(8,128)S(1)} %bitcast.262), channel_id=1, source_target_pairs={{1,0},{2,1},{3,2},{4,3},{5,4},{6,5},{7,6},{0,7},{9,8},{10,9},{11,1... | collective-permute-start | bytes 49160 | tf_op jit(solution)/shard_map/ppermute | solution.py:24
  56.5 2.9 %copy-start.5 = (f32[1,32,512]{2,1,0:T(8,128)S(1)}, f32[1,32,512]{2,1,0:T(8,128)}, u32[]{:S(2)}) copy-start(f32[1,32,512]{2,1,0:T(8,128)} %get-tuple-element.200) | copy-start | bytes 196612
  57.5 19.8 %collective-permute-start.6 = (f32[2,32,1,512]{1,3,2,0:T(8,128)}, f32[2,32,1,512]{1,3,2,0:T(8,128)S(1)}, u32[]{:S(2)}, u32[]{:S(2)}) collective-permute-start(f32[2,32,1,512]{1,3,2,0:T(8,128)} %get-tuple-element.129), channel_id=1, source_target_pairs={{0,8},{8,16},{16,24},{24,32},{32,40},{40,48},{48,56},{56,64},{64,7... | collective-permute-start | bytes 393224 | tf_op jit(solution)/shard_map/ppermute | solution.py:23
  59.8 18.6 %collective-permute-start.7 = (f32[2,32,1,512]{1,3,2,0:T(8,128)S(1)}, f32[2,32,1,512]{1,3,2,0:T(8,128)S(1)}, u32[]{:S(2)}, u32[]{:S(2)}) collective-permute-start(f32[2,32,1,512]{1,3,2,0:T(8,128)S(1)} %get-tuple-element.128), channel_id=1, source_target_pairs={{8,0},{16,8},{24,16},{32,24},{40,32},{48,40},{56,48},{64,56},{72,6... | collective-permute-start | bytes 393224 | tf_op jit(solution)/shard_map/ppermute | solution.py:24
where the time goes:
time: 133 us; the launch traced here: 132 us
  blocking collectives  46 us (35%)
  starting transfers between devices  31.6 us (24%)
  waiting for transfers between devices  23.5 us (18%)
  other arithmetic  19 us (14%)
  local copies, waits for them, and re-layouts  10.6 us (8%)
  between operations  1.4 us (1%)
    psum x4, blocking collectives, over_axes(): array = lax.psum(array, axis)  46 us
    ppermute x4, starting transfers between devices, padded(): after = lax.ppermute(leading, axis, down)  21.4 us
    ppermute x4, waiting for transfers between devices, padded(): before = lax.ppermute(last, axis, up)  19.2 us
    ppermute x4, starting transfers between devices, padded(): before = lax.ppermute(last, axis, up)  10.2 us
    ppermute x4, waiting for transfers between devices, padded(): after = lax.ppermute(leading, axis, down)  4.28 us
  transfers between devices with their start and end apart: 8, of which 6 were waited for; matrix products, arithmetic and copies ran while one was open for 5% of the time, Pallas kernels for 0%

commit v1 on v0

v1 whole, which is shorter than its diff:
```python
import jax
import jax.numpy as jnp
from jax import lax
from jax.experimental import pallas as pl
from jax.experimental.pallas import tpu as pltpu
from jax.sharding import PartitionSpec as P

MESH = pl.DeviceIdType.MESH
SLOTS = 32
LEVELS = 16
GROUPS = 4
CHUNKS = 4
STEPS = 2
Z_RING = 8
count_unit = 4096.0


def row0(base, slot, chunk, col):
    return ((base * SLOTS + slot) * CHUNKS + chunk) * 2 + col


def rows_of(ref, base, group, chunk, col):
    return ref[pl.ds(row0(base, 8 * group, chunk, col), 8, stride=8), :]


def roll(x, shift):
    return pltpu.roll(x, shift % 128, axis=x.ndim - 1)


def make_kernel(nx, ny, z_ring):
    y_ring = nx // z_ring
    rings = (ny, y_ring, z_ring)
    peers = sum(r - 1 for r in rings) + 8
    scale = 1.0 / (nx * 2 * ny * 32 * count_unit)

    def kernel(drop, mov, pair, coll, out, mom, d_in, m_in, p_in, c_in, st, fs, fr, own, rs, rr, code, coef, o_buf, ar,
               in_sem, f_send, f_recv, r_send, r_recv, a_send, a_recv, o_sem):
        gx = lax.axis_index("gx")
        gy = lax.axis_index("gy")
        loads = [
            pltpu.make_async_copy(src, dst, in_sem.at[i])
            for i, (src, dst) in enumerate(((drop, d_in), (mov, m_in), (pair, p_in), (coll, c_in)))
        ]
        for load in loads:
            load.start()

        def at(dx, dy):
            return (lax.rem(gx + dx + nx, nx), lax.rem(gy + dy + ny, ny))

        y_pos = gx // z_ring
        z_pos = lax.rem(gx, z_ring)
        places = (gy, y_pos, z_pos)

        def peer(stage, other):
            if stage == 0:
                return (gx, other)
            if stage == 1:
                return (other * z_ring + z_pos, gy)
            return (y_pos * z_ring + other, gy)

        barrier = pltpu.get_barrier_semaphore()
        for dx in (-1, 0, 1):
            for dy in (-1, 0, 1):
                if dx or dy:
                    pl.semaphore_signal(barrier, inc=1, device_id=at(dx, dy), device_id_type=MESH)
        for stage in range(3):
            for d in range(1, rings[stage]):
                other = lax.rem(places[stage] + d, rings[stage])
                pl.semaphore_signal(barrier, inc=1, device_id=peer(stage, other), device_id_type=MESH)

        lane = lax.broadcasted_iota(jnp.int32, (8, 128), 1)
        lane4 = lax.broadcasted_iota(jnp.int32, (CHUNKS, 8, 128), 2)
        first_row = lane4 < LEVELS
        last_row = lane4 >= 128 - LEVELS
        zero = jnp.zeros((8, 128), jnp.float32)
        copies = []

        def value(step, nm, col, group):
            if step == 0:
                return jnp.stack([rows_of(d_in, nm, group, k, col) for k in range(CHUNKS)])
            return st[nm, col, :, 8 * group : 8 * group + 8, :]

        def codes(step, col, group):
            return jnp.stack([rows_of(m_in, step, group, k, col) for k in range(CHUNKS)])

        def place(down, stay, up):
            up_r = roll(up, LEVELS)
            up_s = jnp.where(first_row, jnp.concatenate([zero[None], up_r[:-1]]), up_r)
            down_r = roll(down, -LEVELS)
            down_s = jnp.where(last_row, jnp.concatenate([down_r[1:], zero[None]]), down_r)
            return stay + up_s + down_s

        def piece(x, k):
            return jnp.where((lane >> 4) == k, x, zero)

        def remote(src, dst, send, recv, target):
            copy = pltpu.make_async_remote_copy(src, dst, send, recv, device_id=target, device_id_type=MESH)
            copy.start()
            copies.append(copy)

        def send_faces(step, nm):
            up_rim = zero
            down_rim = zero
            for g in range(GROUPS):
                for side in range(2):
                    col = 1 - side
                    first = 6 if side == 0 else 0
                    x = value(step, nm, col, g)
                    c = codes(step, col, g)
                    none = jnp.zeros_like(x)
                    down = jnp.where(c == first, x, none)
                    stay = jnp.where(c == first + 1, x, none)
                    up = jnp.where(c == first + 2, x, none)
                    fs[step, nm, side, :, 8 * g : 8 * g + 8, :] = place(down, stay, up)
                    k = side * GROUPS + g
                    up_rim = up_rim + piece(roll(up[CHUNKS - 1], 16 * k + 16), k)
                    down_rim = down_rim + piece(roll(down[0], 16 * k), k)
            rs[step, nm, 2] = up_rim
            rs[step, nm, 3] = down_rim
            for side in range(2):
                remote(fs.at[step, nm, side], fr.at[step, nm, side], f_send.at[step, nm, side], f_recv.at[step, nm, side],
                       at(1 - 2 * side, 0))
            for i in range(4):
                side, down = i // 2, i % 2
                remote(rs.at[step, nm, 2 + down], rr.at[step, nm, 2 + i], r_send.at[step, nm, 2 + i],
                       r_recv.at[step, nm, 2 + i], at(1 - 2 * side, 1 - 2 * down))

        def send_rims(step, nm):
            up_rim = zero
            down_rim = zero
            for g in range(GROUPS):
                x0 = value(step, nm, 0, g)
                x1 = value(step, nm, 1, g)
                c0 = codes(step, 0, g)
                c1 = codes(step, 1, g)
                none = jnp.zeros_like(x0)
                for col in range(2):
                    a = 3 + 3 * col
                    b = 3 * col
                    down = jnp.where(c0 == a, x0, jnp.where(c1 == b, x1, none))
                    stay = jnp.where(c0 == a + 1, x0, jnp.where(c1 == b + 1, x1, none))
                    up = jnp.where(c0 == a + 2, x0, jnp.where(c1 == b + 2, x1, none))
                    own[nm, col, :, 8 * g : 8 * g + 8, :] = place(down, stay, up)
                    k = col * GROUPS + g
                    up_rim = up_rim + piece(roll(up[CHUNKS - 1], 16 * k + 16), k)
                    down_rim = down_rim + piece(roll(down[0], 16 * k), k)
            rs[step, nm, 0] = up_rim
            rs[step, nm, 1] = down_rim
            for down in range(2):
                remote(rs.at[step, nm, down], rr.at[step, nm, down], r_send.at[step, nm, down], r_recv.at[step, nm, down],
                       at(0, 1 - 2 * down))

        def arrived(step, nm):
            for side in range(2):
                f = fs.at[step, nm, side]
                pltpu.make_async_remote_copy(f, fr.at[step, nm, side], f_send.at[step, nm, side], f_recv.at[step, nm, side],
                                             device_id=at(1 - 2 * side, 0), device_id_type=MESH).wait_recv()
            for i in range(6):
                pltpu.make_async_remote_copy(rs.at[step, nm, 0], rr.at[step, nm, i], r_send.at[step, nm, i],
                                             r_recv.at[step, nm, i], device_id=at(0, 1), device_id_type=MESH).wait_recv()
            low = rr[step, nm, 0] + jnp.where(lane < 64, rr[step, nm, 2], rr[step, nm, 4])
            high = rr[step, nm, 1] + jnp.where(lane < 64, rr[step, nm, 3], rr[step, nm, 5])
            return low, high

        def joined(step, nm, col, k, low, high):
            parts = []
            for g in range(GROUPS):
                x = own[nm, col, k, 8 * g : 8 * g + 8, :] + fr[step, nm, col, k, 8 * g : 8 * g + 8, :]
                j = 16 * (col * GROUPS + g)
                if k == 0:
                    x = x + jnp.where(lane < LEVELS, roll(low, -j), zero)
                if k == CHUNKS - 1:
                    x = x + jnp.where(lane >= 128 - LEVELS, roll(high, 112 - j), zero)
                parts.append(x)
            return parts

        def partner_of(parts, c):
            low = c & 7
            high = (c >> 3) & 3
            got = jnp.take_along_axis(parts[0], low, axis=0, mode="promise_in_bounds")
            for g in range(1, GROUPS):
                got = jnp.where(high == g, jnp.take_along_axis(parts[g], low, axis=0, mode="promise_in_bounds"), got)
            return got

        def pair_codes(step):
            def body(i, carry):
                col = i % 2
                k = i // 2
                slot = [lax.broadcasted_iota(jnp.int32, (8, 128), 0) + 8 * g for g in range(GROUPS)]
                acc = [jnp.zeros((8, 128), jnp.int32) for g in range(GROUPS)]
                for p in range(SLOTS // 2):
                    a = jnp.broadcast_to(p_in[pl.ds(row0(step, 2 * p, k, col), 1), :], (8, 128))
                    b = jnp.broadcast_to(p_in[pl.ds(row0(step, 2 * p + 1, k, col), 1), :], (8, 128))
                    g0 = jnp.broadcast_to(c_in[pl.ds(((step * 16 + p) * CHUNKS + k) * 2 + col, 1), :], (8, 128)) * 32
                    for_a = b + g0 + 128
                    for_b = a + g0
                    for g in range(GROUPS):
                        acc[g] = jnp.where(a == slot[g], for_a, jnp.where(b == slot[g], for_b, acc[g]))
                for g in range(GROUPS):
                    code[step, col, k, 8 * g : 8 * g + 8, :] = acc[g]
                return carry

            lax.fori_loop(0, 2 * CHUNKS, body, 0)

        def out_rows(nm, g, k, col, x):
            o_buf[pl.ds(row0(nm, 8 * g, k, col), 8, stride=8), :] = x

        def coalesce_n(step):
            low, high = arrived(step, 0)
            total = zero
            for col in range(2):
                for k in range(CHUNKS):
                    parts = joined(step, 0, col, k, low, high)
                    for g in range(GROUPS):
                        c = code[step, col, k, 8 * g : 8 * g + 8, :]
                        mine = parts[g]
                        other = partner_of(parts, c)
                        g0 = ((c >> 5) & 3).astype(jnp.float32)
                        ahead = jnp.where(c >= 128, 0.5, 0.0)
                        big = jnp.maximum(mine, other)
                        small = jnp.minimum(mine, other)
                        mine_big = mine + ahead > other
                        fits = jnp.where(small * 3.0 <= big, 3.0, jnp.where(small * 2.0 <= big, 2.0, 1.0))
                        taken = jnp.minimum(g0, fits)
                        rest = big - taken * small
                        splits = rest == 0.0
                        half = jnp.floor(small * 0.5)
                        new = jnp.where(mine_big, jnp.where(splits, half, rest), jnp.where(splits, small - half, small))
                        keep = jnp.where(mine_big, jnp.where(splits, taken, 1.0), 1.0)
                        add = jnp.where(mine_big, jnp.where(splits, 1.0, 0.0), taken)
                        coef[0, col, k, 8 * g : 8 * g + 8, :] = keep
                        coef[1, col, k, 8 * g : 8 * g + 8, :] = add
                        st[0, col, k, 8 * g : 8 * g + 8, :] = new
                        total = total + new
                        if step == STEPS - 1:
                            out_rows(0, g, k, col, new)
            return total

        def coalesce_m(step):
            low, high = arrived(step, 1)
            total = zero
            for col in range(2):
                for k in range(CHUNKS):
                    parts = joined(step, 1, col, k, low, high)
                    for g in range(GROUPS):
                        c = code[step, col, k, 8 * g : 8 * g + 8, :]
                        other = partner_of(parts, c)
                        new = coef[0, col, k, 8 * g : 8 * g + 8, :] * parts[g] + coef[1, col, k, 8 * g : 8 * g + 8, :] * other
                        if step < STEPS - 1:
                            st[1, col, k, 8 * g : 8 * g + 8, :] = new
                        else:
                            out_rows(1, g, k, col, new)
                        total = total + st[0, col, k, 8 * g : 8 * g + 8, :] * new
            return total

        loads[0].wait()
        loads[1].wait()
        pl.semaphore_wait(barrier, peers)
        sums = []
        outs = []
        for step in range(STEPS):
            if step == 0:
                send_faces(step, 0)
                send_rims(step, 0)
                send_faces(step, 1)
                send_rims(step, 1)
                loads[2].wait()
                loads[3].wait()
                pair_codes(0)
                pair_codes(1)
            count = coalesce_n(step)
            if step < STEPS - 1:
                send_faces(step + 1, 0)
                send_rims(step + 1, 0)
            else:
                outs.append(pltpu.make_async_copy(o_buf.at[pl.ds(0, 256)], out.at[pl.ds(0, 256)], o_sem.at[0]))
                outs[-1].start()
            liquid = coalesce_m(step)
            if step < STEPS - 1:
                send_faces(step + 1, 1)
                send_rims(step + 1, 1)
            else:
                outs.append(pltpu.make_async_copy(o_buf.at[pl.ds(256, 256)], out.at[pl.ds(256, 256)], o_sem.at[1]))
                outs[-1].start()
            sums.append(jnp.sum(count, axis=0, keepdims=True))
            sums.append(jnp.sum(liquid, axis=0, keepdims=True))
        total = jnp.concatenate(sums, axis=0)
        for stage in range(3):
            place_of = places[stage]
            ar[stage, place_of] = total
            for d in range(1, rings[stage]):
                other = lax.rem(place_of + d, rings[stage])
                remote(ar.at[stage, place_of], ar.at[stage, place_of], a_send.at[stage, d], a_recv.at[stage, place_of],
                       peer(stage, other))
            for d in range(1, rings[stage]):
                other = lax.rem(place_of + d, rings[stage])
                pltpu.make_async_remote_copy(ar.at[stage, other], ar.at[stage, other], a_send.at[stage, d],
                                             a_recv.at[stage, other], device_id=peer(stage, other),
                                             device_id_type=MESH).wait_recv()
            total = ar[stage, 0]
            for d in range(1, rings[stage]):
                total = total + ar[stage, d]
        folded = total
        for d in range(1, 8):
            folded = folded + roll(total, LEVELS * d)
        folded = folded * scale
        for step in range(STEPS):
            mom[step] = folded[2 * step : 2 * step + 2, :LEVELS]
        for copy in copies:
            copy.wait_send()
        for copy in outs:
            copy.wait()

    return kernel


def shards(nx, ny, z_ring):
    def rows(x):
        a, b, cols, flat = x.shape
        x = x.reshape(a, b, cols, CHUNKS, 128).transpose(0, 1, 3, 2, 4)
        return x.reshape(a * b * CHUNKS * cols, 128)

    def step(droplets, moves, pairing, collisions):
        f32 = jnp.float32
        i32 = jnp.int32
        dma = pltpu.SemaphoreType.DMA
        ring = max(ny, nx // z_ring, z_ring)
        hbm = pl.BlockSpec(memory_space=pl.ANY)
        vmem = pl.BlockSpec(memory_space=pltpu.VMEM)
        out, mom = pl.pallas_call(
            make_kernel(nx, ny, z_ring),
            out_shape=(jax.ShapeDtypeStruct((512, 128), f32), jax.ShapeDtypeStruct((STEPS, 2, LEVELS), f32)),
            in_specs=[hbm] * 4,
            out_specs=(hbm, vmem),
            scratch_shapes=[
                pltpu.VMEM((512, 128), f32),
                pltpu.VMEM((512, 128), i32),
                pltpu.VMEM((512, 128), i32),
                pltpu.VMEM((256, 128), i32),
                pltpu.VMEM((2, 2, CHUNKS, SLOTS, 128), f32),
                pltpu.VMEM((STEPS, 2, 2, CHUNKS, SLOTS, 128), f32),
                pltpu.VMEM((STEPS, 2, 2, CHUNKS, SLOTS, 128), f32),
                pltpu.VMEM((2, 2, CHUNKS, SLOTS, 128), f32),
                pltpu.VMEM((STEPS, 2, 4, 8, 128), f32),
                pltpu.VMEM((STEPS, 2, 6, 8, 128), f32),
                pltpu.VMEM((STEPS, 2, CHUNKS, SLOTS, 128), i32),
                pltpu.VMEM((2, 2, CHUNKS, SLOTS, 128), f32),
                pltpu.VMEM((512, 128), f32),
                pltpu.VMEM((3, ring, 4, 128), f32),
                dma((4,)),
                dma((STEPS, 2, 2)),
                dma((STEPS, 2, 2)),
                dma((STEPS, 2, 6)),
                dma((STEPS, 2, 6)),
                dma((3, ring)),
                dma((3, ring)),
                dma((2,)),
            ],
            compiler_params=pltpu.CompilerParams(collective_id=0, has_side_effects=True),
        )(rows(droplets), rows(moves), rows(pairing), rows(collisions))
        out = out.reshape(2, SLOTS, CHUNKS, 2, 128).transpose(0, 1, 3, 2, 4).reshape(droplets.shape)
        return out, mom

    return step


def solution(mesh, z_ring=Z_RING):
    placed = P(None, None, "gx", "gy")
    return jax.shard_map(
        shards(mesh.shape["gx"], mesh.shape["gy"], z_ring), mesh=mesh, in_specs=(placed,) * 4, out_specs=(placed, P()),
        check_vma=False,
    )
```

time: 133 us -> 42.5 us (0.32)
  blocking collectives: 46 us -> 0 us
  Pallas kernels: 0 us -> 39.4 us
  starting transfers between devices: 31.6 us -> 0 us
  waiting for transfers between devices: 23.5 us -> 0 us
  other arithmetic: 19 us -> 0 us
  local copies, waits for them, and re-layouts: 10.6 us -> 2.25 us
    psum x4 -> x0, blocking collectives: 46 us -> none  [over_axes(): array = lax.psum(array, axis)]
    pallas_call x0 -> x1, Pallas kernels: none -> 39.4 us  [step(): pl.pallas_call(make_kernel(nx, ny, z_ring), out_shape=(jax.ShapeDtypeStru...]
    ppermute x8 -> x0, starting transfers between devices: 31.6 us -> none  [the longest x4 21.4 us: padded(): after = lax.ppermute(leading, axis, down)]
    ppermute x8 -> x0, waiting for transfers between devices: 23.5 us -> none  [the longest x4 19.2 us: padded(): before = lax.ppermute(last, axis, up)]
    reduce_sum x22 -> x0, other arithmetic: 6.45 us -> none  [the longest x4 1.7 us: pair_column(): counts_p = jnp.sum(jnp.where(hits, counts[None], 0), axis=1)]
    slice x29 -> x0, local copies, waits for them, and re-layouts: 5.74 us -> none  [the longest x1 1.34 us: coalesce(): order[:, column]]
    another operation x21 -> x0, other arithmetic: 3.32 us -> none  [the longest x6 1.54 us: pair_column(): jnp.stack([first_new, second_new], axis=1).reshape(counts_p.shape)]
    eq x2 -> x0, other arithmetic: 2.26 us -> none  [spread(): chosen = jnp.where((codes == direction)[None], state, jnp.zeros_like(state))]
  transfers between devices with their start and end apart: 8 -> 0, of which waited for: 6 -> 0; matrix products, arithmetic and copies ran while one was open for 5% -> 0% of each run, Pallas kernels for 0% -> 0%
where the time goes in v1:
time: 42.5 us; the launch traced here: 42.3 us
  Pallas kernels  39.4 us (93%)
  local copies, waits for them, and re-layouts  2.25 us (5%)
  between operations  0.65 us (2%)
    pallas_call x1, Pallas kernels, step(): pl.pallas_call(make_kernel(nx, ny, z_ring), out_shape=(jax.ShapeDtypeStru...  39.4 us
    unnamed x4, local copies, waits for them, and re-layouts  2.25 us

profile of v1, /device:TPU:1, one launch (start us, length us, event | category | flops | bytes accessed | tf_op | source)
XLA Modules:
  0.0 42.3 jit_solution(7072410099499648287)
XLA Ops:
  0.6 39.4 %shard_map.59 = (f32[512,128]{1,0:T(8,128)}, f32[2,2,16]{2,1,0:T(2,128)}) custom-call(f32[512,128]{1,0:T(8,128)} %bitcast.25, s32[512,128]{1,0:T(8,128)} %bitcast.26, s32[512,128]{1,0:T(8,128)} %bitcast.27, s32[256,128]{1,0:T(8,128)} %bitcast.29), custom_call_target="tpu_custom_call" | custom-call | tf_op jit(solution)/shard_map/pallas_call | solution.py:330
  40.1 0.0 copy-start
  40.1 1.7 %copy.13 = f32[2,32,2,512]{3,2,1,0:T(2,128)} copy(f32[2,32,2,512]{3,2,1,0:T(2,128)} %bitcast.28) | data formatting | bytes 524288
  41.7 0.0 copy-done
  41.7 0.6 %copy.14 = f32[2,2,16]{2,1,0:T(2,128)} copy(f32[2,2,16]{2,1,0:T(2,128)S(1)} %copy-done) | data formatting | bytes 512
Async XLA Ops:
  40.1 1.7 %copy-start = (f32[2,2,16]{2,1,0:T(2,128)S(1)}, f32[2,2,16]{2,1,0:T(2,128)}, u32[]{:S(2)}) copy-start(f32[2,2,16]{2,1,0:T(2,128)} %get-tuple-element.9) | copy-start | bytes 772

commit v2 on v1

v2 whole, which is shorter than its diff:
```python
import jax
import jax.numpy as jnp
from jax import lax
from jax.experimental import pallas as pl
from jax.experimental.pallas import tpu as pltpu
from jax.sharding import PartitionSpec as P

MESH = pl.DeviceIdType.MESH
SLOTS = 32
PAIRS = 16
LEVELS = 16
GROUPS = 4
CHUNKS = 4
STEPS = 2
Z_RING = 8
count_unit = 4096.0


def row0(base, slot, chunk, col):
    return ((base * SLOTS + slot) * CHUNKS + chunk) * 2 + col


def eight(base, group, chunk, col):
    return pl.ds(row0(base, 8 * group, chunk, col), 8, stride=8)


def roll(x, shift):
    return pltpu.roll(x, shift % 128, axis=x.ndim - 1)


def wrapped(i, d, size):
    j = i + d
    if d > 0:
        return jnp.where(j >= size, j - size, j)
    return jnp.where(j < 0, j + size, j)


def tree_sum(terms):
    while len(terms) > 1:
        terms = [a + b for a, b in zip(terms[::2], terms[1::2])] + ([terms[-1]] if len(terms) % 2 else [])
    return terms[0]


def doublings(size):
    return [1 << i for i in range(10) if (1 << i) < size // 2]


def make_kernel(nx, ny, z_ring):
    y_ring = nx // z_ring
    rounds = [("x", d) for d in doublings(nx)] + [("y", d) for d in doublings(ny)]
    scale = 1.0 / (nx * 2 * ny * 32 * count_unit)

    def hops(d):
        dy, dz = d // z_ring, d % z_ring
        return min(dy, y_ring - dy) + min(dz, z_ring - dz)

    far_first = sorted(range(1, nx), key=lambda d: -hops(d))

    def kernel(drop, mov, pair, coll, out, mom, d_in, m_in, p_in, c_in, st, fs, fr, own, rs, rr, code, coef, ar_y, ar_x,
               in_sem, f_send, f_recv, r_send, r_recv, a_send, a_recv, known):
        gx = lax.axis_index("gx")
        gy = lax.axis_index("gy")
        halves = lambda src, dst, i, n: (src.at[pl.ds(i * n, n)], dst.at[pl.ds(i * n, n)])
        n_load, move_load, m_load, pair_load, coll_load, later_load = [
            pltpu.make_async_copy(src, dst, in_sem.at[i])
            for i, (src, dst) in enumerate(
                (
                    halves(drop, d_in, 0, 256),
                    halves(mov, m_in, 0, 256),
                    halves(drop, d_in, 1, 256),
                    (pair, p_in),
                    (coll, c_in),
                    halves(mov, m_in, 1, 256),
                )
            )
        ]
        n_load.start()
        move_load.start()
        xs = {0: gx, 1: wrapped(gx, 1, nx), -1: wrapped(gx, -1, nx)}
        ys = {0: gy, 1: wrapped(gy, 1, ny), -1: wrapped(gy, -1, ny)}
        barrier = pltpu.get_barrier_semaphore()
        for dx in (-1, 1, 0):
            for dy in (-1, 0, 1):
                if dx or dy:
                    pl.semaphore_signal(barrier, inc=1, device_id=(xs[dx], ys[dy]), device_id_type=MESH)
        m_load.start()
        pair_load.start()
        coll_load.start()
        later_load.start()

        lane = lax.broadcasted_iota(jnp.int32, (8, 128), 1)
        first_row = lane < LEVELS
        last_row = lane >= 128 - LEVELS
        zero = jnp.zeros((8, 128), jnp.float32)
        copies = []

        def tell(i):
            axis, d = rounds[i]
            for e in (d, -d):
                target = (wrapped(gx, e, nx), gy) if axis == "x" else (gx, wrapped(gy, e, ny))
                pl.semaphore_signal(known.at[i], inc=1, device_id=target, device_id_type=MESH)

        def hear(i):
            pl.semaphore_wait(known.at[i], 2)

        def value(step, nm, col, k, g):
            if step == 0:
                return d_in[eight(nm, g, k, col), :]
            return st[nm, col, k, 8 * g : 8 * g + 8, :]

        def moves(step, col, k, g):
            return m_in[eight(step, g, k, col), :]

        def leaving(step, nm, side, k, g):
            x = value(step, nm, 1 - side, k, g)
            c = moves(step, 1 - side, k, g)
            first = 6 if side == 0 else 0
            return [jnp.where(c == first + i, x, zero) for i in range(3)]

        def staying(step, nm, col, k, g):
            x0 = value(step, nm, 0, k, g)
            x1 = value(step, nm, 1, k, g)
            c0 = moves(step, 0, k, g)
            c1 = moves(step, 1, k, g)
            a = 3 + 3 * col
            b = 3 * col
            return [jnp.where(c0 == a + i, x0, jnp.where(c1 == b + i, x1, zero)) for i in range(3)]

        def remote(src, dst, send, recv, target):
            copy = pltpu.make_async_remote_copy(src, dst, send, recv, device_id=target, device_id_type=MESH)
            copy.start()
            copies.append(copy)

        def send_rims(step, nm):
            for kind, part in enumerate((staying, leaving)):
                ups = []
                downs = []
                for i in range(2):
                    for g in range(GROUPS):
                        j = 16 * (i * GROUPS + g)
                        mine = (lane >= j) & (lane < j + 16)
                        ups.append(jnp.where(mine, roll(part(step, nm, i, CHUNKS - 1, g)[2], j + 16), zero))
                        downs.append(jnp.where(mine, roll(part(step, nm, i, 0, g)[0], j), zero))
                rs[step, nm, 2 * kind] = tree_sum(ups)
                rs[step, nm, 2 * kind + 1] = tree_sum(downs)
            for i in range(6):
                side, down = i // 2 - 1, i % 2
                target = (xs[0 if i < 2 else 1 - 2 * side], ys[1 - 2 * down])
                remote(rs.at[step, nm, down + (2 if i >= 2 else 0)], rr.at[step, nm, i], r_send.at[step, nm, i],
                       r_recv.at[step, nm, i], target)

        def send_chunk(step, nm, k):
            for side in range(2):
                remote(fs.at[step, nm, side, k], fr.at[step, nm, side, k], f_send.at[step, nm, side, k],
                       f_recv.at[step, nm, side, k], (xs[1 - 2 * side], gy))

        def send_faces(step, nm, k, held):
            now = {}
            for side in range(2):
                for g in range(GROUPS):
                    down, stay, up = leaving(step, nm, side, k, g)
                    up = roll(up, LEVELS)
                    down = roll(down, -LEVELS)
                    before = zero
                    if k > 0:
                        face, before = held[side, g]
                        fs[step, nm, side, k - 1, 8 * g : 8 * g + 8, :] = face + jnp.where(last_row, down, zero)
                    face = stay + jnp.where(first_row, before, up) + jnp.where(last_row, zero, down)
                    if k == CHUNKS - 1:
                        fs[step, nm, side, k, 8 * g : 8 * g + 8, :] = face
                    now[side, g] = (face, up)
            if k > 0:
                send_chunk(step, nm, k - 1)
            if k == CHUNKS - 1:
                send_chunk(step, nm, k)
            return now

        def keep_own(step, nm):
            for col in range(2):
                for g in range(GROUPS):
                    downs, stays, ups = zip(*[staying(step, nm, col, k, g) for k in range(CHUNKS)])
                    ups = [zero] + [roll(x, LEVELS) for x in ups]
                    downs = [roll(x, -LEVELS) for x in downs] + [zero]
                    for k in range(CHUNKS):
                        own[step, nm, col, k, 8 * g : 8 * g + 8, :] = (
                            stays[k] + jnp.where(first_row, ups[k], ups[k + 1]) + jnp.where(last_row, downs[k + 1], downs[k])
                        )

        def wait_rims(step, nm):
            for i in range(6):
                pltpu.make_async_remote_copy(rs.at[step, nm, 0], rr.at[step, nm, i], r_send.at[step, nm, i],
                                             r_recv.at[step, nm, i], device_id=(gx, ys[1]), device_id_type=MESH).wait_recv()
            low = rr[step, nm, 0] + jnp.where(lane < 64, rr[step, nm, 2], rr[step, nm, 4])
            high = rr[step, nm, 1] + jnp.where(lane < 64, rr[step, nm, 3], rr[step, nm, 5])
            return low, high

        def wait_chunk(step, nm, k):
            for side in range(2):
                pltpu.make_async_remote_copy(fs.at[step, nm, side, k], fr.at[step, nm, side, k], f_send.at[step, nm, side, k],
                                             f_recv.at[step, nm, side, k], device_id=(xs[1], gy),
                                             device_id_type=MESH).wait_recv()

        def joined(step, nm, col, k, rims):
            parts = []
            for g in range(GROUPS):
                x = own[step, nm, col, k, 8 * g : 8 * g + 8, :] + fr[step, nm, col, k, 8 * g : 8 * g + 8, :]
                j = 16 * (col * GROUPS + g)
                if k == 0:
                    x = x + jnp.where(first_row, roll(rims[0], -j), zero)
                if k == CHUNKS - 1:
                    x = x + jnp.where(last_row, roll(rims[1], 112 - j), zero)
                parts.append(x)
            return parts

        def partner_of(parts, c):
            low = c & 7
            high = (c >> 3) & 3
            got = jnp.take_along_axis(parts[0], low, axis=0, mode="promise_in_bounds")
            for g in range(1, GROUPS):
                got = jnp.where(high == g, jnp.take_along_axis(parts[g], low, axis=0, mode="promise_in_bounds"), got)
            return got

        def pair_codes(step):
            def body(i, carry):
                col = i % 2
                k = i // 2
                slot = [lax.broadcasted_iota(jnp.int32, (8, 128), 0) + 8 * g for g in range(GROUPS)]
                acc = [jnp.zeros((8, 128), jnp.int32) for g in range(GROUPS)]
                for p in range(PAIRS):
                    a = jnp.broadcast_to(p_in[pl.ds(row0(step, 2 * p, k, col), 1), :], (8, 128))
                    b = jnp.broadcast_to(p_in[pl.ds(row0(step, 2 * p + 1, k, col), 1), :], (8, 128))
                    g0 = jnp.broadcast_to(c_in[pl.ds(((step * PAIRS + p) * CHUNKS + k) * 2 + col, 1), :], (8, 128)) * 32
                    for_a = b + g0 + 128
                    for_b = a + g0
                    for g in range(GROUPS):
                        acc[g] = jnp.where(a == slot[g], for_a, jnp.where(b == slot[g], for_b, acc[g]))
                for g in range(GROUPS):
                    code[step, col, k, 8 * g : 8 * g + 8, :] = acc[g]
                return carry

            lax.fori_loop(0, 2 * CHUNKS, body, 0)

        def coalesce_n(step, k, rims):
            total = []
            for col in range(2):
                parts = joined(step, 0, col, k, rims)
                for g in range(GROUPS):
                    c = code[step, col, k, 8 * g : 8 * g + 8, :]
                    mine = parts[g]
                    other = partner_of(parts, c)
                    g0 = ((c >> 5) & 3).astype(jnp.float32)
                    ahead = jnp.where(c >= 128, 0.5, 0.0)
                    big = jnp.maximum(mine, other)
                    small = jnp.minimum(mine, other)
                    mine_big = mine + ahead > other
                    fits = jnp.where(small * 3.0 <= big, 3.0, jnp.where(small * 2.0 <= big, 2.0, 1.0))
                    taken = jnp.minimum(g0, fits)
                    rest = big - taken * small
                    splits = rest == 0.0
                    half = jnp.floor(small * 0.5)
                    new = jnp.where(mine_big, jnp.where(splits, half, rest), jnp.where(splits, small - half, small))
                    coef[0, col, k, 8 * g : 8 * g + 8, :] = jnp.where(mine_big, jnp.where(splits, taken, 1.0), 1.0)
                    coef[1, col, k, 8 * g : 8 * g + 8, :] = jnp.where(mine_big, jnp.where(splits, 1.0, 0.0), taken)
                    st[0, col, k, 8 * g : 8 * g + 8, :] = new
                    total.append(new)
                    if step == STEPS - 1:
                        out[eight(0, g, k, col), :] = new
            return tree_sum(total)

        def coalesce_m(step, k, rims):
            total = []
            for col in range(2):
                parts = joined(step, 1, col, k, rims)
                for g in range(GROUPS):
                    c = code[step, col, k, 8 * g : 8 * g + 8, :]
                    other = partner_of(parts, c)
                    new = coef[0, col, k, 8 * g : 8 * g + 8, :] * parts[g] + coef[1, col, k, 8 * g : 8 * g + 8, :] * other
                    if step < STEPS - 1:
                        st[1, col, k, 8 * g : 8 * g + 8, :] = new
                    else:
                        out[eight(1, g, k, col), :] = new
                    total.append(st[0, col, k, 8 * g : 8 * g + 8, :] * new)
            return tree_sum(total)

        def level_row(step, count, liquid, row):
            both = jnp.concatenate([jnp.sum(count, axis=0, keepdims=True), jnp.sum(liquid, axis=0, keepdims=True)], axis=0)
            both = tree_sum([both] + [roll(both, LEVELS * d) for d in range(1, 128 // LEVELS)])
            slot = lane[:1] >> 4
            return jnp.where(slot == 2 * step, both[:1], jnp.where(slot == 2 * step + 1, both[1:], row))

        def both_axes(i):
            n = len(doublings(nx))
            return ([i] if i < n else []) + ([n + i] if n + i < len(rounds) else [])

        def tell_both(i):
            for j in both_axes(i):
                tell(j)

        def hear_both(i):
            for j in both_axes(i):
                hear(j)

        with jax.named_scope("load"):
            n_load.wait()
            move_load.wait()
        with jax.named_scope("barrier"):
            pl.semaphore_wait(barrier, 8)
        with jax.named_scope("send_n"):
            held = send_faces(0, 0, 0, None)
            held = send_faces(0, 0, 1, held)
            send_rims(0, 0)
            held = send_faces(0, 0, 2, held)
            send_faces(0, 0, 3, held)
        with jax.named_scope("send_m"):
            m_load.wait()
            held = send_faces(0, 1, 0, None)
            held = send_faces(0, 1, 1, held)
            send_rims(0, 1)
            held = send_faces(0, 1, 2, held)
            send_faces(0, 1, 3, held)
        with jax.named_scope("own"):
            tell_both(0)
            keep_own(0, 0)
            keep_own(0, 1)
        with jax.named_scope("codes"):
            pair_load.wait()
            coll_load.wait()
            later_load.wait()
            pair_codes(0)
        with jax.named_scope("round"):
            hear_both(0)
            tell_both(1)
        counts = []
        liquids = []
        with jax.named_scope("wait_n"):
            rims = wait_rims(0, 0)
        for k in range(CHUNKS):
            with jax.named_scope("wait_n"):
                wait_chunk(0, 0, k)
            with jax.named_scope("step_n"):
                counts.append(coalesce_n(0, k, rims))
                held = send_faces(1, 0, k, held)
        with jax.named_scope("rims_n"):
            send_rims(1, 0)
        with jax.named_scope("wait_m"):
            rims = wait_rims(0, 1)
        for k in range(CHUNKS):
            with jax.named_scope("wait_m"):
                wait_chunk(0, 1, k)
            with jax.named_scope("step_m"):
                liquids.append(coalesce_m(0, k, rims))
                held = send_faces(1, 1, k, held)
        with jax.named_scope("rims_m"):
            send_rims(1, 1)
        with jax.named_scope("round"):
            hear_both(1)
            tell_both(2)
        with jax.named_scope("own"):
            keep_own(1, 0)
            keep_own(1, 1)
        with jax.named_scope("codes"):
            pair_codes(1)
            row = level_row(0, tree_sum(counts), tree_sum(liquids), jnp.zeros((1, 128), jnp.float32))
        with jax.named_scope("wait_n"):
            rims = wait_rims(1, 0)
            for k in range(CHUNKS):
                wait_chunk(1, 0, k)
        with jax.named_scope("coalesce_n"):
            count = tree_sum([coalesce_n(1, k, rims) for k in range(CHUNKS)])
        with jax.named_scope("round"):
            hear_both(2)
            tell_both(3)
        with jax.named_scope("wait_m"):
            rims = wait_rims(1, 1)
            for k in range(CHUNKS):
                wait_chunk(1, 1, k)
        with jax.named_scope("coalesce_m"):
            liquid = tree_sum([coalesce_m(1, k, rims) for k in range(CHUNKS)])
            row = level_row(1, count, liquid, row)

        def all_send(buf, sem, n):
            return pltpu.make_async_remote_copy(buf.at[pl.ds(0, n)], buf.at[pl.ds(0, n)], a_send.at[sem], a_recv.at[sem],
                                                device_id=(gx, ys[1]), device_id_type=MESH)

        with jax.named_scope("reduce_y"):
            ar_y[gy] = row
            for d in range(1, ny):
                pltpu.make_async_remote_copy(ar_y.at[gy], ar_y.at[gy], a_send.at[0], a_recv.at[0],
                                             device_id=(gx, wrapped(gy, d, ny)), device_id_type=MESH).start()
            for i in range(3, max(len(doublings(nx)), 4)):
                hear_both(i)
                tell_both(i + 1)
            all_send(ar_y, 0, ny - 1).wait_recv()
            row = tree_sum([ar_y[i] for i in range(ny)])
        with jax.named_scope("send_x"):
            ar_x[gx] = row
            for d in far_first:
                pltpu.make_async_remote_copy(ar_x.at[gx], ar_x.at[gx], a_send.at[1], a_recv.at[1],
                                             device_id=(wrapped(gx, d, nx), gy), device_id_type=MESH).start()
        with jax.named_scope("reduce_x"):
            all_send(ar_x, 1, nx - 1).wait_recv()
            row = tree_sum([ar_x[i] for i in range(nx)]) * scale
        with jax.named_scope("tail"):
            for step in range(STEPS):
                for i in range(2):
                    mom[step, i : i + 1, :] = roll(row, -LEVELS * (2 * step + i))[:, :LEVELS]
            for copy in copies:
                copy.wait_send()
            all_send(ar_y, 0, ny - 1).wait_send()
            all_send(ar_x, 1, nx - 1).wait_send()

    return kernel


def write_out(out_v, mom_v, out, mom, sem):
    first = pltpu.make_async_copy(out_v, out, sem.at[0])
    second = pltpu.make_async_copy(mom_v, mom, sem.at[1])
    first.start()
    second.start()
    first.wait()
    second.wait()


def shards(nx, ny, z_ring):
    def rows(x):
        a, b, cols, flat = x.shape
        x = x.reshape(a, b, cols, CHUNKS, 128).transpose(0, 1, 3, 2, 4)
        return x.reshape(a * b * CHUNKS * cols, 128)

    def step(droplets, moves, pairing, collisions):
        f32 = jnp.float32
        i32 = jnp.int32
        dma = pltpu.SemaphoreType.DMA
        hbm = pl.BlockSpec(memory_space=pl.ANY)
        vmem = pl.BlockSpec(memory_space=pltpu.VMEM)
        faces = pltpu.VMEM((STEPS, 2, 2, CHUNKS, SLOTS, 128), f32)
        pairs = (2, 2, CHUNKS, SLOTS, 128)
        n_known = len(doublings(nx)) + len(doublings(ny))
        out, mom = pl.pallas_call(
            make_kernel(nx, ny, z_ring),
            out_shape=(pltpu.VMEM((512, 128), f32), pltpu.VMEM((STEPS, 2, LEVELS), f32)),
            in_specs=[hbm] * 4,
            out_specs=(vmem, vmem),
            scratch_shapes=[
                pltpu.VMEM((512, 128), f32),
                pltpu.VMEM((512, 128), i32),
                pltpu.VMEM((512, 128), i32),
                pltpu.VMEM((256, 128), i32),
                pltpu.VMEM(pairs, f32),
                faces,
                faces,
                faces,
                pltpu.VMEM((STEPS, 2, 4, 8, 128), f32),
                pltpu.VMEM((STEPS, 2, 6, 8, 128), f32),
                pltpu.VMEM(pairs, i32),
                pltpu.VMEM(pairs, f32),
                pltpu.VMEM((ny, 1, 128), f32),
                pltpu.VMEM((nx, 1, 128), f32),
                dma((6,)),
                dma((STEPS, 2, 2, CHUNKS)),
                dma((STEPS, 2, 2, CHUNKS)),
                dma((STEPS, 2, 6)),
                dma((STEPS, 2, 6)),
                dma((2,)),
                dma((2,)),
                pltpu.SemaphoreType.REGULAR((max(n_known, 1),)),
            ],
            compiler_params=pltpu.CompilerParams(collective_id=0, has_side_effects=True),
        )(rows(droplets), rows(moves), rows(pairing), rows(collisions))
        out, mom = pl.pallas_call(
            write_out,
            out_shape=(jax.ShapeDtypeStruct((512, 128), f32), jax.ShapeDtypeStruct((STEPS, 2, LEVELS), f32)),
            in_specs=[vmem, vmem],
            out_specs=(hbm, hbm),
            scratch_shapes=[dma((2,))],
        )(pltpu.with_memory_space_constraint(out, pltpu.VMEM), pltpu.with_memory_space_constraint(mom, pltpu.VMEM))
        out = out.reshape(2, SLOTS, CHUNKS, 2, 128).transpose(0, 1, 3, 2, 4).reshape(droplets.shape)
        return out, mom

    return step


def solution(mesh, z_ring=Z_RING):
    placed = P(None, None, "gx", "gy")
    return jax.shard_map(
        shards(mesh.shape["gx"], mesh.shape["gy"], z_ring), mesh=mesh, in_specs=(placed,) * 4, out_specs=(placed, P()),
        check_vma=False,
    )
```

time: 42.5 us -> 37.8 us (0.89)
  Pallas kernels: 39.4 us -> 37 us
  local copies, waits for them, and re-layouts: 2.25 us -> 0 us
    pallas_call x1 -> x2, Pallas kernels: 39.4 us -> 37 us  [the longest x1 36.3 us: step(): pl.pallas_call(make_kernel(nx, ny, z_ring), out_shape=(pltpu.VMEM((512, 1...]
    unnamed x4 -> x0, local copies, waits for them, and re-layouts: 2.25 us -> none
where the time goes in v2:
time: 37.8 us; the launch traced here: 37.6 us
  Pallas kernels  37 us (98%)
  between operations  0.64 us (2%)
    pallas_call x1, Pallas kernels, step(): pl.pallas_call(make_kernel(nx, ny, z_ring), out_shape=(pltpu.VMEM((512, 1...  36.3 us

profile of v2, /device:TPU:1, one launch (start us, length us, event | category | flops | bytes accessed | tf_op | source)
XLA Modules:
  0.0 37.6 jit_solution(7545177170258505522)
XLA Ops:
  0.6 36.3 %shard_map.59 = (f32[512,128]{1,0:T(8,128)S(1)}, f32[2,2,16]{2,1,0:T(2,128)S(1)}) custom-call(f32[512,128]{1,0:T(8,128)} %bitcast.25, s32[512,128]{1,0:T(8,128)} %bitcast.26, s32[512,128]{1,0:T(8,128)} %bitcast.27, s32[256,128]{1,0:T(8,128)} %bitcast.28), custom_call_target="tpu_custom_call" | custom-call | tf_op jit(solution)/shard_map/pallas_call | solution.py:439
  36.9 0.7 %shard_map.60 = (f32[512,128]{1,0:T(8,128)}, f32[2,2,16]{2,1,0:T(2,128)}) custom-call(f32[512,128]{1,0:T(8,128)S(1)} %get-tuple-element.6.out_v, f32[2,2,16]{2,1,0:T(2,128)S(1)} %get-tuple-element.7.mom_v), custom_call_target="tpu_custom_call" | custom-call | tf_op jit(solution)/shard_map/pallas_call | solution.py:470

commit v3 on v2

v3 whole, which is shorter than its diff:
```python
import jax
import jax.numpy as jnp
from jax import lax
from jax.experimental import pallas as pl
from jax.experimental.pallas import tpu as pltpu
from jax.sharding import PartitionSpec as P

MESH = pl.DeviceIdType.MESH
SLOTS = 32
PAIRS = 16
LEVELS = 16
GROUPS = 4
CHUNKS = 4
STEPS = 2
Z_RING = 8
ORDER = (0, 3, 1, 2)
count_unit = 4096.0


def rim(step, nm):
    return 6 * nm if step == 0 else 12 + 10 * nm


def row0(base, slot, chunk, col):
    return ((base * SLOTS + slot) * CHUNKS + chunk) * 2 + col


def eight(base, group, chunk, col):
    return pl.ds(row0(base, 8 * group, chunk, col), 8, stride=8)


def roll(x, shift):
    return pltpu.roll(x, shift % 128, axis=x.ndim - 1)


def wrapped(i, d, size):
    j = i + d
    if d > 0:
        return jnp.where(j >= size, j - size, j)
    return jnp.where(j < 0, j + size, j)


def tree_sum(terms):
    while len(terms) > 1:
        terms = [a + b for a, b in zip(terms[::2], terms[1::2])] + ([terms[-1]] if len(terms) % 2 else [])
    return terms[0]


def doublings(size):
    return [1 << i for i in range(10) if (1 << i) < size // 2]


def make_kernel(nx, ny, z_ring):
    y_ring = nx // z_ring
    along_x = [z_ring * d for d in doublings(y_ring)] + doublings(z_ring)
    along_y = doublings(ny)
    scale = 1.0 / (nx * 2 * ny * 32 * count_unit)

    def hops(d):
        dy, dz = d // z_ring, d % z_ring
        return min(dy, y_ring - dy) + min(dz, z_ring - dz)

    far_first = sorted(range(1, nx), key=lambda d: -hops(d))

    def kernel(drop, mov, pair, coll, out, mom, d_in, m_in, p_in, c_in, st, fs, fr, own, rs, rr, code, coef, ar_y, ar_x,
               in_sem, send_sem, f_recv, r_recv, a_recv, known):
        gx = lax.axis_index("gx")
        gy = lax.axis_index("gy")
        halves = lambda src, dst, i, n: (src.at[pl.ds(i * n, n)], dst.at[pl.ds(i * n, n)])
        n_load, move_load, m_load, pair_load, coll_load, later_load = [
            pltpu.make_async_copy(src, dst, in_sem.at[i])
            for i, (src, dst) in enumerate(
                (
                    halves(drop, d_in, 0, 256),
                    halves(mov, m_in, 0, 256),
                    halves(drop, d_in, 1, 256),
                    (pair, p_in),
                    (coll, c_in),
                    halves(mov, m_in, 1, 256),
                )
            )
        ]
        n_load.start()
        move_load.start()
        xs = {0: gx, 1: wrapped(gx, 1, nx), -1: wrapped(gx, -1, nx)}
        ys = {0: gy, 1: wrapped(gy, 1, ny), -1: wrapped(gy, -1, ny)}
        barrier = pltpu.get_barrier_semaphore()
        greeted = [(xs[dx], ys[dy]) for dx, dy in ((-1, -1), (-1, 1), (1, -1), (1, 1), (-1, 0), (1, 0), (0, -1), (0, 1))]
        greeted += [(wrapped(gx, z_ring, nx), gy), (wrapped(gx, -z_ring, nx), gy)]
        for target in greeted:
            pl.semaphore_signal(barrier, inc=1, device_id=target, device_id_type=MESH)
        m_load.start()
        pair_load.start()
        coll_load.start()
        later_load.start()

        lane = lax.broadcasted_iota(jnp.int32, (8, 128), 1)
        first_row = lane < LEVELS
        last_row = lane >= 128 - LEVELS
        zero = jnp.zeros((8, 128), jnp.float32)

        def tell(i):
            targets = []
            if i < len(along_x):
                targets += [(wrapped(gx, e * along_x[i], nx), gy) for e in (1, -1)]
            if i < len(along_y):
                targets += [(gx, wrapped(gy, e * along_y[i], ny)) for e in (1, -1)]
            for target in targets:
                pl.semaphore_signal(known.at[i], inc=1, device_id=target, device_id_type=MESH)

        def hear(i):
            heard = 2 * (i < len(along_x)) + 2 * (i < len(along_y))
            if heard:
                pl.semaphore_wait(known.at[i], heard)

        def value(step, nm, col, k, g):
            if step == 0:
                return d_in[eight(nm, g, k, col), :]
            return st[nm, col, k, 8 * g : 8 * g + 8, :]

        def moves(step, col, k, g):
            return m_in[eight(step, g, k, col), :]

        def leaving(step, nm, side, k, g):
            x = value(step, nm, 1 - side, k, g)
            c = moves(step, 1 - side, k, g)
            first = 6 if side == 0 else 0
            return [jnp.where(c == first + i, x, zero) for i in range(3)]

        def staying(step, nm, col, k, g):
            x0 = value(step, nm, 0, k, g)
            x1 = value(step, nm, 1, k, g)
            c0 = moves(step, 0, k, g)
            c1 = moves(step, 1, k, g)
            a = 3 + 3 * col
            b = 3 * col
            return [jnp.where(c0 == a + i, x0, jnp.where(c1 == b + i, x1, zero)) for i in range(3)]

        def remote(src, dst, send, recv, target):
            pltpu.make_async_remote_copy(src, dst, send_sem.at[send], recv, device_id=target, device_id_type=MESH).start()

        def send_rims(step, nm, down):
            for kind, part in enumerate((staying, leaving)):
                pieces = []
                for i in range(2):
                    for g in range(GROUPS):
                        j = 16 * (i * GROUPS + g)
                        x = part(step, nm, i, 0 if down else CHUNKS - 1, g)[0 if down else 2]
                        pieces.append(jnp.where((lane >= j) & (lane < j + 16), roll(x, j if down else j + 16), zero))
                rs[step, nm, 2 * kind + down] = tree_sum(pieces)
                for side in range(kind + 1):
                    target = (xs[1 - 2 * side if kind else 0], ys[1 - 2 * down])
                    remote(rs.at[step, nm, 2 * kind + down], rr.at[rim(step, nm) + 2 * (kind + side) + down], 1, r_recv.at[step, nm],
                           target)

        def face_sem(step, nm, k):
            return f_recv.at[nm * CHUNKS + k if step == 0 else 2 * CHUNKS + nm]

        def send_face(step, nm, k):
            for side in range(2):
                remote(fs.at[step, nm, k, side], fr.at[step, nm, k, side], 0, face_sem(step, nm, k), (xs[1 - 2 * side], gy))

        def send_faces(nm, then):
            parts = {}

            def get(side, g, k):
                if (side, g, k) not in parts:
                    down, stay, up = leaving(0, nm, side, k, g)
                    parts[side, g, k] = (roll(down, -LEVELS), stay, roll(up, LEVELS))
                return parts[side, g, k]

            for k in ORDER:
                for side in range(2):
                    for g in range(GROUPS):
                        down, stay, up = get(side, g, k)
                        before = get(side, g, k - 1)[2] if k > 0 else zero
                        after = get(side, g, k + 1)[0] if k < CHUNKS - 1 else zero
                        fs[0, nm, k, side, 8 * g : 8 * g + 8, :] = (
                            stay + jnp.where(first_row, before, up) + jnp.where(last_row, after, down)
                        )
                send_face(0, nm, k)
                if k == ORDER[0]:
                    then()

        def send_part(nm, k, held):
            patches = []
            for side in range(2):
                pieces = []
                for g in range(GROUPS):
                    down, stay, up = leaving(1, nm, side, k, g)
                    down_r = roll(down, -LEVELS)
                    up_r = roll(up, LEVELS)
                    before = held[side, g, k - 1][2] if (side, g, k - 1) in held else zero
                    after = held[side, g, k + 1][0] if (side, g, k + 1) in held else zero
                    held[side, g, k] = (down_r, stay, up_r)
                    fs[1, nm, k, side, 8 * g : 8 * g + 8, :] = (
                        stay + jnp.where(first_row, before, up_r) + jnp.where(last_row, after, down_r)
                    )
                    if k in (1, 2):
                        j = 16 * g
                        pieces.append(jnp.where((lane >= j) & (lane < j + 16), roll(down, j), zero))
                    if k == 2:
                        j = 64 + 16 * g
                        pieces.append(jnp.where((lane >= j) & (lane < j + 16), roll(up, j + 16), zero))
                if pieces:
                    patches.append(tree_sum(pieces))
            send_face(1, nm, k)
            for side, patch in enumerate(patches):
                i = 2 * (k - 1) + side
                rs[1, nm, 4 + i] = patch
                remote(rs.at[1, nm, 4 + i], rr.at[rim(1, nm) + 6 + i], 1, r_recv.at[1, nm], (xs[1 - 2 * side], gy))

        def keep_own(step, nm):
            for col in range(2):
                for g in range(GROUPS):
                    downs, stays, ups = zip(*[staying(step, nm, col, k, g) for k in range(CHUNKS)])
                    ups = [zero] + [roll(x, LEVELS) for x in ups]
                    downs = [roll(x, -LEVELS) for x in downs] + [zero]
                    for k in range(CHUNKS):
                        own[step, nm, col, k, 8 * g : 8 * g + 8, :] = (
                            stays[k] + jnp.where(first_row, ups[k], ups[k + 1]) + jnp.where(last_row, downs[k + 1], downs[k])
                        )

        def arrived(buf, sem):
            pltpu.make_async_remote_copy(buf, buf, send_sem.at[0], sem, device_id=(gx, ys[1]), device_id_type=MESH).wait_recv()

        def wait_rims(step, nm):
            arrived(rr.at[pl.ds(rim(step, nm), 6 if step == 0 else 10)], r_recv.at[step, nm])
            low = rr[rim(step, nm) + 0] + jnp.where(lane < 64, rr[rim(step, nm) + 2], rr[rim(step, nm) + 4])
            high = rr[rim(step, nm) + 1] + jnp.where(lane < 64, rr[rim(step, nm) + 3], rr[rim(step, nm) + 5])
            return low, high

        def joined(step, nm, col, k, rims):
            parts = []
            for g in range(GROUPS):
                x = own[step, nm, col, k, 8 * g : 8 * g + 8, :] + fr[step, nm, k, col, 8 * g : 8 * g + 8, :]
                j = 16 * (col * GROUPS + g)
                if k == 0:
                    x = x + jnp.where(first_row, roll(rims[0], -j), zero)
                if k == CHUNKS - 1:
                    x = x + jnp.where(last_row, roll(rims[1], 112 - j), zero)
                if step > 0 and k < 2:
                    x = x + jnp.where(last_row, roll(rr[rim(step, nm) + 6 + 2 * k + col], 112 - 16 * g), zero)
                if step > 0 and k == 3:
                    x = x + jnp.where(first_row, roll(rr[rim(step, nm) + 8 + col], -64 - 16 * g), zero)
                parts.append(x)
            return parts

        def partner_of(parts, c):
            low = c & 7
            high = (c >> 3) & 3
            got = jnp.take_along_axis(parts[0], low, axis=0, mode="promise_in_bounds")
            for g in range(1, GROUPS):
                got = jnp.where(high == g, jnp.take_along_axis(parts[g], low, axis=0, mode="promise_in_bounds"), got)
            return got

        def pair_codes(step):
            def body(i, carry):
                col = i % 2
                k = i // 2
                slot = [lax.broadcasted_iota(jnp.int32, (8, 128), 0) + 8 * g for g in range(GROUPS)]
                acc = [jnp.zeros((8, 128), jnp.int32) for g in range(GROUPS)]
                for p in range(PAIRS):
                    a = jnp.broadcast_to(p_in[pl.ds(row0(step, 2 * p, k, col), 1), :], (8, 128))
                    b = jnp.broadcast_to(p_in[pl.ds(row0(step, 2 * p + 1, k, col), 1), :], (8, 128))
                    g0 = jnp.broadcast_to(c_in[pl.ds(((step * PAIRS + p) * CHUNKS + k) * 2 + col, 1), :], (8, 128)) * 32
                    for_a = b + g0 + 128
                    for_b = a + g0
                    for g in range(GROUPS):
                        acc[g] = jnp.where(a == slot[g], for_a, jnp.where(b == slot[g], for_b, acc[g]))
                for g in range(GROUPS):
                    code[step, col, k, 8 * g : 8 * g + 8, :] = acc[g]
                return carry

            lax.fori_loop(0, 2 * CHUNKS, body, 0)

        def coalesce_n(step, k, rims):
            total = []
            for col in range(2):
                parts = joined(step, 0, col, k, rims)
                for g in range(GROUPS):
                    c = code[step, col, k, 8 * g : 8 * g + 8, :]
                    mine = parts[g]
                    other = partner_of(parts, c)
                    g0 = ((c >> 5) & 3).astype(jnp.float32)
                    ahead = jnp.where(c >= 128, 0.5, 0.0)
                    big = jnp.maximum(mine, other)
                    small = jnp.minimum(mine, other)
                    mine_big = mine + ahead > other
                    fits = jnp.where(small * 3.0 <= big, 3.0, jnp.where(small * 2.0 <= big, 2.0, 1.0))
                    taken = jnp.minimum(g0, fits)
                    rest = big - taken * small
                    splits = rest == 0.0
                    half = jnp.floor(small * 0.5)
                    new = jnp.where(mine_big, jnp.where(splits, half, rest), jnp.where(splits, small - half, small))
                    coef[0, col, k, 8 * g : 8 * g + 8, :] = jnp.where(mine_big, jnp.where(splits, taken, 1.0), 1.0)
                    coef[1, col, k, 8 * g : 8 * g + 8, :] = jnp.where(mine_big, jnp.where(splits, 1.0, 0.0), taken)
                    st[0, col, k, 8 * g : 8 * g + 8, :] = new
                    total.append(new)
                    if step == STEPS - 1:
                        out[eight(0, g, k, col), :] = new
            return tree_sum(total)

        def coalesce_m(step, k, rims):
            total = []
            for col in range(2):
                parts = joined(step, 1, col, k, rims)
                for g in range(GROUPS):
                    c = code[step, col, k, 8 * g : 8 * g + 8, :]
                    other = partner_of(parts, c)
                    new = coef[0, col, k, 8 * g : 8 * g + 8, :] * parts[g] + coef[1, col, k, 8 * g : 8 * g + 8, :] * other
                    if step < STEPS - 1:
                        st[1, col, k, 8 * g : 8 * g + 8, :] = new
                    else:
                        out[eight(1, g, k, col), :] = new
                    total.append(st[0, col, k, 8 * g : 8 * g + 8, :] * new)
            return tree_sum(total)

        def fold(x):
            x = jnp.sum(x, axis=0, keepdims=True)
            return tree_sum([x] + [roll(x, LEVELS * d) for d in range(1, 128 // LEVELS)])

        slot = lane[:1] >> 4
        row = jnp.zeros((1, 128), jnp.float32)
        with jax.named_scope("load"):
            n_load.wait()
            move_load.wait()
        with jax.named_scope("barrier"):
            pl.semaphore_wait(barrier, len(greeted))
        for nm in range(2):
            with jax.named_scope("send"):
                if nm == 1:
                    m_load.wait()

                def both_rims(nm=nm):
                    for down in (1, 0):
                        send_rims(0, nm, down)
                    if nm == 0:
                        tell(0)

                send_faces(nm, both_rims)
        with jax.named_scope("own"):
            keep_own(0, 0)
            keep_own(0, 1)
        with jax.named_scope("codes"):
            pair_load.wait()
            coll_load.wait()
            later_load.wait()
            pair_codes(0)
        with jax.named_scope("round"):
            hear(0)
            tell(1)
        for nm, coalesce in enumerate((coalesce_n, coalesce_m)):
            with jax.named_scope("wait_rims"):
                rims = wait_rims(0, nm)
            held = {}
            sums = []
            for k in ORDER:
                with jax.named_scope("wait_face"):
                    arrived(fr.at[0, nm, k], face_sem(0, nm, k))
                with jax.named_scope("step"):
                    sums.append(coalesce(0, k, rims))
                    send_part(nm, k, held)
                    if k in (0, CHUNKS - 1):
                        send_rims(1, nm, int(k == 0))
            row = jnp.where(slot == nm, fold(tree_sum(sums)), row)
            if nm == 0:
                with jax.named_scope("round"):
                    hear(1)
                    tell(2)
        with jax.named_scope("own"):
            keep_own(1, 0)
            keep_own(1, 1)
        with jax.named_scope("codes"):
            pair_codes(1)
        for nm, coalesce in enumerate((coalesce_n, coalesce_m)):
            with jax.named_scope("wait_last"):
                arrived(fr.at[1, nm], face_sem(1, nm, 0))
                rims = wait_rims(1, nm)
            with jax.named_scope("coalesce"):
                total = tree_sum([coalesce(1, k, rims) for k in range(CHUNKS)])
                row = jnp.where(slot == 2 + nm, fold(total), row)
            if nm == 0:
                with jax.named_scope("round"):
                    hear(2)
                    tell(3)
        with jax.named_scope("reduce_y"):
            ar_y[gy] = row
            for d in range(1, ny):
                remote(ar_y.at[gy], ar_y.at[gy], 2, a_recv.at[0], (gx, wrapped(gy, d, ny)))
            hear(3)
            arrived(ar_y.at[pl.ds(0, ny - 1)], a_recv.at[0])
            row = tree_sum([ar_y[i] for i in range(ny)])
        with jax.named_scope("send_x"):
            ar_x[gx] = row
            for d in far_first:
                remote(ar_x.at[gx], ar_x.at[gx], 3, a_recv.at[1], (wrapped(gx, d, nx), gy))
        with jax.named_scope("reduce_x"):
            arrived(ar_x.at[pl.ds(0, nx - 1)], a_recv.at[1])
            row = tree_sum([ar_x[i] for i in range(nx)]) * scale
        with jax.named_scope("tail"):
            for step in range(STEPS):
                for i in range(2):
                    mom[step, i : i + 1, :] = roll(row, -LEVELS * (2 * step + i))[:, :LEVELS]
            for i, sent in enumerate((fs, rr, ar_y.at[pl.ds(0, ny - 1)], ar_x.at[pl.ds(0, nx - 1)])):
                pltpu.make_async_remote_copy(sent, sent, send_sem.at[i], f_recv.at[0], device_id=(gx, ys[1]),
                                             device_id_type=MESH).wait_send()

    return kernel


def write_out(out_v, mom_v, out, mom, sem):
    first = pltpu.make_async_copy(out_v, out, sem.at[0])
    second = pltpu.make_async_copy(mom_v, mom, sem.at[1])
    first.start()
    second.start()
    first.wait()
    second.wait()


def shards(nx, ny, z_ring):
    def rows(x):
        a, b, cols, flat = x.shape
        x = x.reshape(a, b, cols, CHUNKS, 128).transpose(0, 1, 3, 2, 4)
        return x.reshape(a * b * CHUNKS * cols, 128)

    def step(droplets, moves, pairing, collisions):
        f32 = jnp.float32
        i32 = jnp.int32
        dma = pltpu.SemaphoreType.DMA
        hbm = pl.BlockSpec(memory_space=pl.ANY)
        vmem = pl.BlockSpec(memory_space=pltpu.VMEM)
        faces = pltpu.VMEM((STEPS, 2, CHUNKS, 2, SLOTS, 128), f32)
        kept = pltpu.VMEM((STEPS, 2, 2, CHUNKS, SLOTS, 128), f32)
        pairs = (2, 2, CHUNKS, SLOTS, 128)
        out, mom = pl.pallas_call(
            make_kernel(nx, ny, z_ring),
            out_shape=(pltpu.VMEM((512, 128), f32), pltpu.VMEM((STEPS, 2, LEVELS), f32)),
            in_specs=[hbm] * 4,
            out_specs=(vmem, vmem),
            scratch_shapes=[
                pltpu.VMEM((512, 128), f32),
                pltpu.VMEM((512, 128), i32),
                pltpu.VMEM((512, 128), i32),
                pltpu.VMEM((256, 128), i32),
                pltpu.VMEM(pairs, f32),
                faces,
                faces,
                kept,
                pltpu.VMEM((STEPS, 2, 8, 8, 128), f32),
                pltpu.VMEM((32, 8, 128), f32),
                pltpu.VMEM(pairs, i32),
                pltpu.VMEM(pairs, f32),
                pltpu.VMEM((ny, 1, 128), f32),
                pltpu.VMEM((nx, 1, 128), f32),
                dma((6,)),
                dma((4,)),
                dma((2 * CHUNKS + 2,)),
                dma((STEPS, 2)),
                dma((2,)),
                pltpu.SemaphoreType.REGULAR((4,)),
            ],
            compiler_params=pltpu.CompilerParams(collective_id=0, has_side_effects=True),
        )(rows(droplets), rows(moves), rows(pairing), rows(collisions))
        out, mom = pl.pallas_call(
            write_out,
            out_shape=(jax.ShapeDtypeStruct((512, 128), f32), jax.ShapeDtypeStruct((STEPS, 2, LEVELS), f32)),
            in_specs=[vmem, vmem],
            out_specs=(hbm, hbm),
            scratch_shapes=[dma((2,))],
        )(pltpu.with_memory_space_constraint(out, pltpu.VMEM), pltpu.with_memory_space_constraint(mom, pltpu.VMEM))
        out = out.reshape(2, SLOTS, CHUNKS, 2, 128).transpose(0, 1, 3, 2, 4).reshape(droplets.shape)
        return out, mom

    return step


def solution(mesh, z_ring=Z_RING):
    placed = P(None, None, "gx", "gy")
    return jax.shard_map(
        shards(mesh.shape["gx"], mesh.shape["gy"], z_ring), mesh=mesh, in_specs=(placed,) * 4, out_specs=(placed, P()),
        check_vma=False,
    )
```

time: 37.8 us -> 36.5 us (0.966)
  Pallas kernels: 37 us -> 35.7 us
    pallas_call x1, Pallas kernels: 36.3 us -> 35 us  [step(): pl.pallas_call(make_kernel(nx, ny, z_ring), out_shape=(pltpu.VMEM((512, 1...]
where the time goes in v3:
time: 36.5 us; the launch traced here: 36.4 us
  Pallas kernels  35.7 us (98%)
  between operations  0.64 us (2%)
    pallas_call x1, Pallas kernels, step(): pl.pallas_call(make_kernel(nx, ny, z_ring), out_shape=(pltpu.VMEM((512, 1...  35 us

profile of v3, /device:TPU:1, one launch (start us, length us, event | category | flops | bytes accessed | tf_op | source)
XLA Modules:
  0.0 36.4 jit_solution(9376028946545374523)
XLA Ops:
  0.6 35.0 %shard_map.59 = (f32[512,128]{1,0:T(8,128)S(1)}, f32[2,2,16]{2,1,0:T(2,128)S(1)}) custom-call(f32[512,128]{1,0:T(8,128)} %bitcast.25, s32[512,128]{1,0:T(8,128)} %bitcast.26, s32[512,128]{1,0:T(8,128)} %bitcast.27, s32[256,128]{1,0:T(8,128)} %bitcast.28), custom_call_target="tpu_custom_call" | custom-call | tf_op jit(solution)/shard_map/pallas_call | solution.py:436
  35.7 0.7 %shard_map.60 = (f32[512,128]{1,0:T(8,128)}, f32[2,2,16]{2,1,0:T(2,128)}) custom-call(f32[512,128]{1,0:T(8,128)S(1)} %get-tuple-element.6.out_v, f32[2,2,16]{2,1,0:T(2,128)S(1)} %get-tuple-element.7.mom_v), custom_call_target="tpu_custom_call" | custom-call | tf_op jit(solution)/shard_map/pallas_call | solution.py:465
